TPU v7x, 32 devices: a 4x4x1 block of a 4x4x8 slice. The times are simulated.
32 devices in a mesh: dp: 1 (over z), ey: 4 (over y), ex: 8 (over x, core).
Axes of the slice: x: 4, y: 4, z: 1, core: 2. Of those that a mesh axis runs over, the one named last changes fastest.
The devices are a block of a 4x4x8 slice.
Arguments:
- x: bfloat16 [16384, 2048], P(('dp', 'ey', 'ex'))
- ids: int32 [16384, 8], P(('dp', 'ey', 'ex'))
- gates: float32 [16384, 8], P(('dp', 'ey', 'ex'))
- w1: bfloat16 [64, 2048, 1024], P(('ey', 'ex'))
- w3: bfloat16 [64, 2048, 1024], P(('ey', 'ex'))
- w2: bfloat16 [64, 1024, 2048], P(('ey', 'ex'))
Outputs:
- output: bfloat16 [16384, 2048], P(('dp', 'ey', 'ex'))
All inputs are finite; a program needn't handle non-finite values.
Results may differ from a plain program's by a relative error of at most 0.00589437.
Values are sent between devices in bfloat16 or wider.
A program may use at most 768 MiB of HBM per device.

v0:
```python
import jax
import jax.numpy as jnp
from jax import lax
from jax.sharding import PartitionSpec as P

CAPF = 2


def solution(mesh):
    nx = mesh.shape["ex"]
    nd = mesh.shape["ey"] * nx
    axes = ("ey", "ex")
    tok = P(("dp", "ey", "ex"), None)
    wsp = P(("ey", "ex"), None, None)

    def local(x, ids, gates, w1, w3, w2):
        t, hd = x.shape
        top = ids.shape[1]
        el = w1.shape[0]
        cap = min(t, CAPF * t * top // nd)
        me = lax.axis_index("ey") * nx + lax.axis_index("ex")
        dev = ids // el
        hit = jnp.any(dev[:, :, None] == jnp.arange(nd)[None, None, :], axis=1)
        rank = jnp.cumsum(hit.astype(jnp.int32), axis=0) - 1
        kept = hit & (rank < cap)
        slot = jnp.where(kept, rank, cap)
        dst = jnp.broadcast_to(jnp.arange(nd)[None, :], (t, nd))
        src = jnp.broadcast_to(jnp.arange(t)[:, None], (t, nd))
        sx = jnp.zeros((nd, cap, hd), x.dtype).at[dst, slot].set(x[src], mode="drop")
        si = jnp.full((nd, cap, top), -1, jnp.int32).at[dst, slot].set(ids[src], mode="drop")
        sg = jnp.zeros((nd, cap, top), jnp.float32).at[dst, slot].set(gates[src], mode="drop")
        rx = lax.all_to_all(sx, axes, 0, 0, tiled=True).reshape(nd * cap, hd)
        ri = lax.all_to_all(si, axes, 0, 0, tiled=True).reshape(nd * cap, top)
        rg = lax.all_to_all(sg, axes, 0, 0, tiled=True).reshape(nd * cap, top)
        a1 = jnp.einsum("rh,ehf->erf", rx, w1, preferred_element_type=jnp.float32)
        a3 = jnp.einsum("rh,ehf->erf", rx, w3, preferred_element_type=jnp.float32)
        hh = (jax.nn.silu(a1) * a3).astype(jnp.bfloat16)
        o = jnp.einsum("erf,efh->erh", hh, w2, preferred_element_type=jnp.float32).astype(jnp.bfloat16)
        eid = me * el + jnp.arange(el)
        coef = jnp.sum(jnp.where(ri[None, :, :] == eid[:, None, None], rg[None, :, :], 0.0), axis=2)
        part = jnp.sum(coef[:, :, None] * o, axis=0).reshape(nd, cap, hd)
        back = lax.all_to_all(part, axes, 0, 0, tiled=True)
        got = back[dst, jnp.minimum(slot, cap - 1)]
        moe_out = jnp.sum(jnp.where(kept[:, :, None], got, 0.0), axis=1)
        return (x.astype(jnp.float32) + moe_out).astype(jnp.bfloat16)

    return jax.shard_map(local, mesh=mesh, in_specs=(tok, tok, tok, wsp, wsp, wsp),
                         out_specs=tok, check_vma=False)
```

profile of v0, /device:TPU:96, one launch (start us, length us, event | category | flops | bytes accessed | tf_op | source)
XLA Modules:
  0.0 2636.7 jit_solution(531010321263397875)
XLA Ops:
  0.0 0.8 add_select_fusion
  0.8 0.1 fusion.20
  0.9 0.0 copy-start.4
  0.9 1.2 reduce-window.6
  2.1 0.2 slice_reduce_fusion
  2.3 0.1 fusion.21
  2.5 0.5 copy-done.10
  2.9 0.7 and_reduce_fusion
  3.7 0.7 multiply_reduce_fusion.1
  4.4 0.0 copy-done.4
  4.5 0.1 copy.50
  4.6 0.1 reshape.97
  4.7 0.8 copy.53
  5.6 0.1 reshape.69
  5.7 0.0 copy-done.2
  5.7 0.0 copy-start
  5.8 98.9 %scatter_custom_fusion.1 = f32[8192,8]{1,0:T(8,128)} fusion(s32[16384]{0:T(1024)S(1)} %reshape.97, f32[512,8]{1,0:T(8,128)S(1)} %copy.53, s32[16384]{0:T(1024)S(1)} %broadcast_clamp_fusion.1, f32[]{:T(128)} %constant.47.clone.1), kind=kCustom, calls=%fused_computation.22 | custom fusion | bytes 262148
  104.6 3.5 copy.54
  108.1 8.1 all-to-all-start.1
  116.2 0.1 copy.51
  116.3 7.8 sort
  124.1 98.9 %scatter_custom_fusion = s32[8192,8]{1,0:T(8,128)} fusion(s32[16384]{0:T(1024)S(1)} %reshape.97, s32[512,8]{1,0:T(8,128)S(1)} %copy.51, s32[16384]{0:T(1024)S(1)} %broadcast_clamp_fusion.1, s32[]{:T(128)} %constant.21.clone.1), kind=kCustom, calls=%fused_computation.24 | custom fusion | bytes 262148
  223.0 3.4 copy.52
  226.5 80.3 %gather_fusion = bf16[16384,2048]{1,0:T(8,128)(2,1)} fusion(bf16[512,2048]{1,0:T(8,128)(2,1)S(1)} %copy-done, s32[16384]{0:T(1024)S(1)} %broadcast_clamp_fusion.1), kind=kCustom, calls=%fused_computation.2 | custom fusion | bytes 134283264 | tf_op jit(solution)/shard_map/gather | solution.py:29
  306.8 0.0 all-to-all-done.1
  306.8 6.7 all-to-all-start
  313.6 304.7 %scatter_custom_fusion.2 = bf16[8192,2048]{1,0:T(8,128)(2,1)} fusion(s32[16384]{0:T(1024)} %get-tuple-element.5, bf16[16384,2048]{1,0:T(8,128)(2,1)} %gather_fusion, s32[16384]{0:T(1024)S(1)} %broadcast_clamp_fusion, bf16[]{:T(256)} %constant.48.clone.1), kind=kCustom, calls=%fused_computation.10 | custom fusion | bytes 33554944
  618.3 0.0 all-to-all-done
  618.3 6.5 all-to-all-start.2
  624.8 1.8 select_reduce_fusion.1
  626.7 437.2 %all-to-all-done.2 = bf16[32,256,2048]{2,1,0:T(8,128)(2,1)} async-done(((bf16[32,256,2048]{2,1,0:T(8,128)(2,1)}), bf16[32,256,2048]{2,1,0:T(8,128)(2,1)}, u32[]{:S(2)}, u32[]{:S(2)}) %all-to-all-start.2) | async-done | bytes 33554464 | tf_op jit(solution)/shard_map/all_to_all | solution.py:32
  1063.9 78.4 %fusion.32 = f32[8192,2,1024]{2,0,1:T(8,128)} fusion(bf16[8192,2048,1]{1,0,2:T(8,128)(2,1)} %bitcast.9, bf16[2,2048,1024]{2,1,0:T(8,128)(2,1)} %param.9), kind=kOutput, calls=%fused_computation.62 | convolution fusion | flops 68719476736 | bytes 109051904 | tf_op jit(solution)/shard_map/rh,ehf->erf/dot_general | solution.py:35
  1142.3 82.9 %fusion.47 = bf16[2,8192,1024]{2,1,0:T(8,128)(2,1)} fusion(f32[8192,2,1024]{2,0,1:T(8,128)} %fusion.32, bf16[8192,2048,1]{1,0,2:T(8,128)(2,1)} %bitcast.9, bf16[2,2048,1024]{2,1,0:T(8,128)(2,1)} %param.10), kind=kOutput, calls=%fused_computation.13.clone.clone.1 | convolution fusion | flops 68820140032 | bytes 142606336 | tf_op jit(solution)/shard_map/rh,ehf->erf/dot_general | solution.py:36
  1225.2 93.3 %multiply_reduce_fusion = f32[8192,2048]{1,0:T(8,128)} fusion(f32[2,8192]{1,0:T(2,128)S(1)} %copy-done.9, bf16[2,1024,2048]{2,1,0:T(8,128)(2,1)} %param.11, bf16[2,8192,1024]{2,1,0:T(8,128)(2,1)} %fusion.47), kind=kOutput, calls=%fused_computation.9 | convolution fusion | flops 68836917248 | bytes 109117440 | tf_op jit(solution)/shard_map/erf,efh->erh/dot_general | solution.py:38
  1318.4 6.2 all-to-all-start.3
  1324.6 0.0 copy-done.3
  1324.6 0.0 copy-done.5
  1324.6 0.0 copy-done.11
  1324.6 0.1 fusion.28
  1324.7 0.8 copy.49
  1325.5 0.1 fusion.25
  1325.6 0.1 copy.55
  1325.8 0.1 reshape.91
  1325.9 857.4 %all-to-all-done.3 = f32[32,256,2048]{2,1,0:T(8,128)} async-done(((f32[32,256,2048]{2,1,0:T(8,128)}), f32[32,256,2048]{2,1,0:T(8,128)}, u32[]{:S(2)}, u32[]{:S(2)}) %all-to-all-start.3) | async-done | bytes 67108896 | tf_op jit(solution)/shard_map/all_to_all | solution.py:42
  2183.3 409.9 %gather_fusion.1 = f32[16384,2048]{1,0:T(8,128)} fusion(f32[32,256,2048]{2,1,0:T(8,128)} %all-to-all-done.3, s32[16384]{0:T(1024)S(1)} %reshape.91), kind=kCustom, calls=%fused_computation.3 | custom fusion | bytes 268566528 | tf_op jit(solution)/shard_map/gather | solution.py:43
  2593.2 41.1 %select_reduce_fusion = f32[512,2048]{1,0:T(8,128)S(1)} fusion(pred[512,32]{1,0:T(8,128)(4,1)S(1)} %copy-done.6, f32[16384,2048]{1,0:T(8,128)} %gather_fusion.1), kind=kLoop, calls=%fused_computation.8 | loop fusion | flops 66060288 | bytes 138428416 | tf_op jit(solution)/shard_map/reduce_sum | solution.py:44
  2634.3 0.0 copy-done.1
  2634.3 2.0 add_convert_fusion
  (25 shorter events, 0.1 us)
Async XLA Ops:
  0.0 116.2 %copy-start.7 = (s32[512,8]{0,1:T(8,128)S(1)}, s32[512,8]{0,1:T(8,128)}, u32[]{:S(2)}) copy-start(s32[512,8]{0,1:T(8,128)} %param.7) | copy-start | bytes 49156
  0.9 3.6 copy-start.4
  2.1 3.6 copy-start.2
  2.3 0.6 copy-start.10
  5.7 220.7 %copy-start = (bf16[512,2048]{1,0:T(8,128)(2,1)S(1)}, bf16[512,2048]{1,0:T(8,128)(2,1)}, u32[]{:S(2)}) copy-start(bf16[512,2048]{1,0:T(8,128)(2,1)} %param.6) | copy-start | bytes 6291460
  108.1 198.7 %all-to-all-start.1 = ((f32[32,256,8]{1,2,0:T(8,128)}), f32[32,256,8]{1,2,0:T(8,128)}, u32[]{:S(2)}, u32[]{:S(2)}) async-start(f32[32,256,8]{1,2,0:T(8,128)} %bitcast.5), calls=%async_computation.1 | async-start | bytes 524288 | tf_op jit(solution)/shard_map/all_to_all | solution.py:34
  226.5 87.1 %copy-start.8 = (s32[16384]{0:T(1024)S(1)}, s32[16384]{0:T(1024)}, u32[]{:S(2)}) copy-start(s32[16384]{0:T(1024)} %get-tuple-element.6) | copy-start | bytes 196612
  306.8 311.5 %all-to-all-start = ((s32[32,256,8]{1,2,0:T(8,128)}), s32[32,256,8]{1,2,0:T(8,128)S(1)}, u32[]{:S(2)}, u32[]{:S(2)}) async-start(s32[32,256,8]{1,2,0:T(8,128)} %bitcast.3), calls=%async_computation | async-start | bytes 524288 | tf_op jit(solution)/shard_map/all_to_all | solution.py:33
  618.3 445.6 %all-to-all-start.2 = ((bf16[32,256,2048]{2,1,0:T(8,128)(2,1)}), bf16[32,256,2048]{2,1,0:T(8,128)(2,1)}, u32[]{:S(2)}, u32[]{:S(2)}) async-start(bf16[32,256,2048]{2,1,0:T(8,128)(2,1)} %bitcast.103), calls=%async_computation.2 | async-start | bytes 67108864 | tf_op jit(solution)/shard_map/all_to_all | solution.py:32
  1142.3 82.9 %copy-start.9 = (f32[2,8192]{1,0:T(2,128)S(1)}, f32[2,8192]{1,0:T(2,128)}, u32[]{:S(2)}) copy-start(f32[2,8192]{1,0:T(2,128)} %select_reduce_fusion.1) | copy-start | bytes 196612
  1318.4 6.2 copy-start.3
  1318.4 6.2 copy-start.5
  1318.4 6.2 copy-start.11
  1318.4 864.9 %all-to-all-start.3 = ((f32[32,256,2048]{2,1,0:T(8,128)}), f32[32,256,2048]{2,1,0:T(8,128)}, u32[]{:S(2)}, u32[]{:S(2)}) async-start(f32[32,256,2048]{2,1,0:T(8,128)} %bitcast.13), calls=%async_computation.3 | async-start | bytes 134217728 | tf_op jit(solution)/shard_map/all_to_all | solution.py:42
  2183.3 409.9 %copy-start.6 = (pred[512,32]{1,0:T(8,128)(4,1)S(1)}, pred[512,32]{1,0:T(8,128)(4,1)}, u32[]{:S(2)}) copy-start(pred[512,32]{1,0:T(8,128)(4,1)} %copy.49) | copy-start | bytes 49156
  2593.2 41.1 %copy-start.1 = (bf16[512,2048]{1,0:T(8,128)(2,1)S(1)}, bf16[512,2048]{1,0:T(8,128)(2,1)}, u32[]{:S(2)}) copy-start(bf16[512,2048]{1,0:T(8,128)(2,1)} %param.6) | copy-start | bytes 6291460
where the time goes:
time: 2650 us; the launch traced here: 2640 us
  waiting for transfers between devices  1290 us (49%)
  local copies, waits for them, and re-layouts  1000 us (38%)
  matrix products  255 us (10%)
  other arithmetic  56.6 us (2%)
  starting transfers between devices  27.5 us (1%)
    all_to_all x1, waiting for transfers between devices, local(): back = lax.all_to_all(part, axes, 0, 0, tiled=True)  857 us
    unnamed x34, local copies, waits for them, and re-layouts  511 us
    all_to_all x1, waiting for transfers between devices, local(): rx = lax.all_to_all(sx, axes, 0, 0, tiled=True).reshape(nd * cap, hd)  437 us
    gather x1, local copies, waits for them, and re-layouts, local(): got = back[dst, jnp.minimum(slot, cap - 1)]  410 us
    dot_general x1, matrix products, local(): jnp.einsum('erf,efh->erh', hh, w2, preferred_element_type=jnp.float32)  93.3 us
    dot_general x1, matrix products, local(): a3 = jnp.einsum('rh,ehf->erf', rx, w3, preferred_element_type=jnp.float32)  82.9 us
    gather x1, local copies, waits for them, and re-layouts, local(): x[src]  80.3 us
    dot_general x1, matrix products, local(): a1 = jnp.einsum('rh,ehf->erf', rx, w1, preferred_element_type=jnp.float32)  78.4 us
  transfers between devices with their start and end apart: 4, of which 2 were waited for; matrix products, arithmetic and copies ran while one was open for 19% of the time, Pallas kernels for 0%

commit v1 on v0

v1 whole, which is shorter than its diff:
```python
import jax
import jax.numpy as jnp
from jax import lax
from jax.experimental import pallas as pl
from jax.experimental.pallas import tpu as pltpu
from jax.sharding import PartitionSpec as P

CAPF = 2
CHUNKS = 4
BLOCK = 512
TILE = 256


def expert_kernel(cnt, row_ref, col_ref, x_ref, w1_ref, w3_ref, w2_ref, o_ref):
    b = pl.program_id(0)
    el = w1_ref.shape[0]
    blk = x_ref.shape[0]
    o_ref[...] = jnp.zeros_like(o_ref)
    for e in range(el):
        n = cnt[b * el + e]

        def tile(i, carry):
            base = i * TILE
            rows = lax.broadcasted_iota(jnp.int32, (TILE, blk), 0) + base
            pick = jnp.where(row_ref[0, e:e + 1, :] == rows.astype(jnp.float32), 1.0, 0.0).astype(jnp.bfloat16)
            xs = jnp.dot(pick, x_ref[...], preferred_element_type=jnp.float32).astype(jnp.bfloat16)
            a1 = jnp.dot(xs, w1_ref[e], preferred_element_type=jnp.float32)
            a3 = jnp.dot(xs, w3_ref[e], preferred_element_type=jnp.float32)
            h = (jax.nn.silu(a1) * a3).astype(jnp.bfloat16)
            o = jnp.dot(h, w2_ref[e], preferred_element_type=jnp.float32).astype(jnp.bfloat16)
            cols = lax.broadcasted_iota(jnp.int32, (blk, TILE), 1) + base
            put = jnp.where(col_ref[0, :, e:e + 1] == cols.astype(jnp.float32), 1.0, 0.0).astype(jnp.bfloat16)
            s = jnp.dot(put, o, preferred_element_type=jnp.float32)
            o_ref[...] += col_ref[0, :, el + e:el + e + 1] * s
            return carry

        lax.fori_loop(0, (n + TILE - 1) // TILE, tile, 0)


def experts(cnt, rowp, colp, xg, w1, w3, w2):
    n, hd = xg.shape
    nb, el, blk = rowp.shape
    f = w1.shape[2]
    whole = lambda b, c: (0, 0, 0)
    once = pl.Buffered(1)
    return pl.pallas_call(
        expert_kernel,
        out_shape=jax.ShapeDtypeStruct((n, hd), jnp.float32),
        grid_spec=pltpu.PrefetchScalarGridSpec(
            num_scalar_prefetch=1,
            grid=(nb,),
            in_specs=[
                pl.BlockSpec((1, el, blk), lambda b, c: (b, 0, 0)),
                pl.BlockSpec((1, blk, colp.shape[2]), lambda b, c: (b, 0, 0)),
                pl.BlockSpec((blk, hd), lambda b, c: (b, 0)),
                pl.BlockSpec(w1.shape, whole, pipeline_mode=once),
                pl.BlockSpec(w3.shape, whole, pipeline_mode=once),
                pl.BlockSpec(w2.shape, whole, pipeline_mode=once),
            ],
            out_specs=pl.BlockSpec((blk, hd), lambda b, c: (b, 0)),
        ),
        compiler_params=pltpu.CompilerParams(vmem_limit_bytes=60 * 1024 * 1024),
        cost_estimate=pl.CostEstimate(
            flops=2 * 3 * n * hd * f, transcendentals=n * f, bytes_accessed=6 * n * hd + 6 * el * hd * f),
        name="experts",
    )(cnt, rowp, colp, xg, w1, w3, w2)


def solution(mesh):
    nx = mesh.shape["ex"]
    nd = mesh.shape["ey"] * nx
    axes = ("ey", "ex")
    tok = P(("dp", "ey", "ex"), None)
    wsp = P(("ey", "ex"), None, None)

    def local(x, ids, gates, w1, w3, w2):
        t, hd = x.shape
        top = ids.shape[1]
        el = w1.shape[0]
        cap = min(t, CAPF * t * top // nd)
        ct = t // CHUNKS
        xs = [lax.all_gather(x[c * ct:(c + 1) * ct], axes, axis=0, tiled=True) for c in range(CHUNKS)]

        eid = jnp.arange(nd * el)[:, None]
        coef = jnp.full((nd * el, t), -1.0, jnp.float32)
        for j in range(top):
            coef = jnp.where(ids[:, j][None, :] == eid, gates[:, j][None, :], coef)
        hit = jnp.any((coef >= 0).reshape(nd, el, t), axis=1)
        upto = (jnp.arange(t)[:, None] <= jnp.arange(t)[None, :]).astype(jnp.bfloat16)
        rank = jnp.dot(hit.astype(jnp.bfloat16), upto, preferred_element_type=jnp.float32)
        kept = hit & (rank <= cap)
        coef = jnp.where(kept[:, None, :], coef.reshape(nd, el, t), -1.0)
        mine = lax.all_to_all(coef, axes, 0, 0, tiled=True)

        spb = BLOCK // ct
        nb = nd // spb
        c4 = mine.reshape(nb, spb, el, CHUNKS, ct).transpose(3, 0, 2, 1, 4).reshape(CHUNKS, nb, el, BLOCK)
        sel = c4 >= 0
        within = (jnp.arange(BLOCK)[:, None] <= jnp.arange(BLOCK)[None, :]).astype(jnp.bfloat16)
        cum = jnp.dot(sel.reshape(-1, BLOCK).astype(jnp.bfloat16), within,
                      preferred_element_type=jnp.float32).reshape(sel.shape)
        place = jnp.where(sel, cum - 1.0, -1.0)
        counts = cum[..., -1].astype(jnp.int32).reshape(CHUNKS, nb * el)
        colp = jnp.concatenate([place, c4], axis=2).transpose(0, 1, 3, 2)

        outs = []
        for c in range(CHUNKS):
            part = experts(counts[c], place[c], colp[c], xs[c], w1, w3, w2)
            back = lax.psum_scatter(part, axes, scatter_dimension=0, tiled=True)
            outs.append((x[c * ct:(c + 1) * ct].astype(jnp.float32) + back).astype(jnp.bfloat16))
        return jnp.concatenate(outs, axis=0)

    return jax.shard_map(local, mesh=mesh, in_specs=(tok, tok, tok, wsp, wsp, wsp),
                         out_specs=tok, check_vma=False)
```

time: 2650 us -> 950 us (0.36)
  the two profiles are of different devices: /device:TPU:96 before, /device:TPU:97 now
where the time goes in v1:
time: 950 us; the launch traced here: 943 us
  waiting for transfers between devices  484 us (51%)
  Pallas kernels  352 us (37%)
  local copies, waits for them, and re-layouts  42 us (4%)
  other arithmetic  32.5 us (3%)
  blocking collectives  17.6 us (2%)
  between operations  13.9 us (1%)
    reduce_scatter x4, waiting for transfers between devices, local(): back = lax.psum_scatter(part, axes, scatter_dimension=0, tiled=True)  482 us
    pallas_call x4, Pallas kernels, experts(): pl.pallas_call(expert_kernel, out_shape=jax.ShapeDtypeStruct((n, hd), jnp...  352 us
    squeeze x10, local copies, waits for them, and re-layouts, local(): part = experts(counts[c], place[c], colp[c], xs[c], w1, w3, w2)  24.2 us
  transfers between devices with their start and end apart: 8, of which 3 were waited for; matrix products, arithmetic and copies ran while one was open for 7% of the time, Pallas kernels for 37%

profile of v1, /device:TPU:97, one launch (start us, length us, event | category | flops | bytes accessed | tf_op | source)
XLA Modules:
  0.0 943.0 jit_solution(8974967923767432433)
XLA Ops:
  6.6 3.0 fusion.4
  9.6 0.1 all-gather.9.cloned.1.call-start
  9.6 0.7 all-gather.9.cloned.1.call-update
  10.4 0.1 all-gather.7.cloned.1.call-start
  10.5 0.7 all-gather.7.cloned.1.call-update
  11.3 0.6 all-gather.5.cloned.1.call-update
  11.8 0.1 reduce-scatter.11.cloned.1.call-start
  12.0 0.5 compare_reduce_fusion
  12.5 0.2 fusion
  12.7 0.1 broadcast_select_fusion
  12.8 17.6 %all_to_all.5 = f32[32,2,512]{2,1,0:T(2,128)S(1)} all-to-all(f32[32,2,512]{2,1,0:T(2,128)S(1)} %broadcast_select_fusion), channel_id=1, replica_groups=mesh['dp'=1,'ey'=4,'ex'=8] {'ey','ex'}, dimensions={0} | all-to-all | bytes 262144 | tf_op jit(solution)/shard_map/all_to_all | solution.py:93
  30.4 0.1 reshape.265
  30.6 4.6 copy.40
  35.2 4.7 broadcast_compare_fusion
  39.9 2.7 copy.41
  42.6 0.2 fusion.2
  42.8 4.7 copy.43
  47.5 11.2 %add_select_fusion = f32[4,8,2,512]{2,3,1,0:T(8,128)} fusion(f32[4,8,2,512]{2,3,1,0:T(8,128)} %copy.43, f32[4,8,2,4,128]{2,4,3,1,0:T(8,128)} %copy.40), kind=kLoop, calls=%fused_computation.1 | loop fusion | flops 98304 | bytes 393216 | tf_op jit(solution)/shard_map/jit(_where)/select_n | solution.py:102
  58.7 6.6 slice_bitcast_fusion.7
  65.3 2.8 copy.50.row_ref
  68.1 0.1 slice_convert_fusion
  68.2 0.6 fusion.5
  68.8 0.1 copy.49
  69.0 0.6 squeeze.46.cnt
  69.5 11.5 %maximum_bitcast_fusion = f32[4,8,512,4]{3,2,1,0:T(8,128)} fusion(f32[4,8,2,512]{2,3,1,0:T(8,128)} %bitcast.63, f32[4,8,2,512]{2,3,1,0:T(8,128)} %add_select_fusion), kind=kLoop, calls=%fused_computation | loop fusion | flops 65536 | bytes 524288 | tf_op jit(solution)/shard_map/transpose | solution.py:104
  81.1 6.9 slice_bitcast_fusion.6
  88.0 87.4 %experts.7 = f32[4096,2048]{1,0:T(8,128)} custom-call(s32[16]{0:T(128)} %squeeze.46.cnt, f32[8,2,512]{2,1,0:T(2,128)} %copy.50.row_ref, f32[8,512,4]{2,1,0:T(8,128)} %get-tuple-element.8.col_ref, bf16[4096,2048]{1,0:T(8,128)(2,1)} %all-gather.11.cloned.1.call-done.x_ref, bf16[2,2048,1024]{2,1,0:T(8,128)(2,1)} %w1_ref.7, bf16[2,2048,1024]{2,1,0:T(8,128)(2,1)} %w3_ref.7, ...), custom_call_target="tpu_custom_call" | custom-call | flops 51539607552 | bytes 75497472 | tf_op jit(solution)/shard_map/experts/pallas_call | solution.py:46
  175.5 0.1 reduce-scatter.9.cloned.1.call-start
  175.5 2.8 copy.48.row_ref
  178.4 0.1 copy.47
  178.5 0.7 squeeze.43.cnt
  179.2 88.8 %experts.6 = f32[4096,2048]{1,0:T(8,128)} custom-call(s32[16]{0:T(128)} %squeeze.43.cnt, f32[8,2,512]{2,1,0:T(2,128)} %copy.48.row_ref, f32[8,512,4]{2,1,0:T(8,128)} %get-tuple-element.9.col_ref, bf16[4096,2048]{1,0:T(8,128)(2,1)} %all-gather.9.cloned.1.call-done.x_ref, bf16[2,2048,1024]{2,1,0:T(8,128)(2,1)} %w1_ref.7, bf16[2,2048,1024]{2,1,0:T(8,128)(2,1)} %w3_ref.7, ...), custom_call_target="tpu_custom_call" | custom-call | flops 51539607552 | bytes 75497472 | tf_op jit(solution)/shard_map/experts/pallas_call | solution.py:46
  268.0 0.1 reduce-scatter.7.cloned.1.call-start
  268.1 1.2 copy.46.row_ref
  269.4 0.1 copy.45
  269.5 0.7 squeeze.40.cnt
  270.2 87.7 %experts.5 = f32[4096,2048]{1,0:T(8,128)} custom-call(s32[16]{0:T(128)} %squeeze.40.cnt, f32[8,2,512]{2,1,0:T(2,128)} %copy.46.row_ref, f32[8,512,4]{2,1,0:T(8,128)} %get-tuple-element.10.col_ref, bf16[4096,2048]{1,0:T(8,128)(2,1)} %all-gather.7.cloned.1.call-done.x_ref, bf16[2,2048,1024]{2,1,0:T(8,128)(2,1)} %w1_ref.7, bf16[2,2048,1024]{2,1,0:T(8,128)(2,1)} %w3_ref.7, ...), custom_call_target="tpu_custom_call" | custom-call | flops 51539607552 | bytes 75497472 | tf_op jit(solution)/shard_map/experts/pallas_call | solution.py:46
  357.9 0.1 reduce-scatter.5.cloned.1.call-start
  358.0 1.5 copy-done.1
  359.5 1.2 copy.44.row_ref
  360.7 0.1 copy.42
  360.9 0.7 squeeze.37.cnt
  361.5 87.8 %experts.4 = f32[4096,2048]{1,0:T(8,128)} custom-call(s32[16]{0:T(128)} %squeeze.37.cnt, f32[8,2,512]{2,1,0:T(2,128)} %copy.44.row_ref, f32[8,512,4]{2,1,0:T(8,128)} %get-tuple-element.7.col_ref, bf16[4096,2048]{1,0:T(8,128)(2,1)} %all-gather.5.cloned.1.call-done.x_ref, bf16[2,2048,1024]{2,1,0:T(8,128)(2,1)} %w1_ref.7, bf16[2,2048,1024]{2,1,0:T(8,128)(2,1)} %w3_ref.7, ...), custom_call_target="tpu_custom_call" | custom-call | flops 51539607552 | bytes 75497472 | tf_op jit(solution)/shard_map/experts/pallas_call | solution.py:46
  449.4 160.6 %reduce-scatter.9.cloned.1.call-done = f32[128,2048]{1,0:T(8,128)} async-done(((f32[4096,2048]{1,0:T(8,128)}), f32[128,2048]{1,0:T(8,128)}) %reduce-scatter.9.cloned.1.call-update) | async-done | bytes 1048592 | tf_op jit(solution)/shard_map/reduce_scatter | solution.py:109
  610.0 160.7 %reduce-scatter.7.cloned.1.call-done = f32[128,2048]{1,0:T(8,128)} async-done(((f32[4096,2048]{1,0:T(8,128)}), f32[128,2048]{1,0:T(8,128)}) %reduce-scatter.7.cloned.1.call-update) | async-done | bytes 1048592 | tf_op jit(solution)/shard_map/reduce_scatter | solution.py:109
  770.7 160.7 %reduce-scatter.5.cloned.1.call-done = f32[128,2048]{1,0:T(8,128)} async-done(((f32[4096,2048]{1,0:T(8,128)}), f32[128,2048]{1,0:T(8,128)}) %reduce-scatter.5.cloned.1.call-update) | async-done | bytes 1048592 | tf_op jit(solution)/shard_map/reduce_scatter | solution.py:109
  931.5 2.8 add_convert_fusion.3
  934.3 1.6 pad_maximum_fusion
  (24 shorter events, 0.4 us)
Async XLA Ops:
  6.5 5.4 copy-start.3
  6.5 5.4 copy-start.4
  6.6 81.4 %all-gather.11.cloned.1.call-start = ((), (), s32[]{:S(2)}) async-start(), calls=%async_computation.11 | async-start | bytes 17301504 | tf_op jit(solution)/shard_map/all_gather | solution.py:82
  9.6 169.6 %all-gather.9.cloned.1.call-start = ((), (), s32[]{:S(2)}) async-start(), calls=%async_computation.9 | async-start | bytes 17301504 | tf_op jit(solution)/shard_map/all_gather | solution.py:82
  10.4 259.8 %all-gather.7.cloned.1.call-start = ((), (), s32[]{:S(2)}) async-start(), calls=%async_computation.7 | async-start | bytes 17301504 | tf_op jit(solution)/shard_map/all_gather | solution.py:82
  11.2 350.3 %all-gather.5.cloned.1.call-start = ((), (), s32[]{:S(2)}) async-start(), calls=%async_computation.5 | async-start | bytes 17301504 | tf_op jit(solution)/shard_map/all_gather | solution.py:82
  11.8 437.6 %reduce-scatter.11.cloned.1.call-start = ((), (), s32[]{:S(2)}) async-start(), calls=%async_computation.12 | async-start | bytes 34603008 | tf_op jit(solution)/shard_map/reduce_scatter | solution.py:109
  175.5 434.5 %reduce-scatter.9.cloned.1.call-start = ((), (), s32[]{:S(2)}) async-start(), calls=%async_computation.10 | async-start | bytes 34603008 | tf_op jit(solution)/shard_map/reduce_scatter | solution.py:109
  268.0 502.7 %reduce-scatter.7.cloned.1.call-start = ((), (), s32[]{:S(2)}) async-start(), calls=%async_computation.8 | async-start | bytes 34603008 | tf_op jit(solution)/shard_map/reduce_scatter | solution.py:109
  357.8 1.7 copy-start.1
  357.8 2.9 copy-start.2
  357.9 573.6 %reduce-scatter.5.cloned.1.call-start = ((), (), s32[]{:S(2)}) async-start(), calls=%async_computation.6 | async-start | bytes 34603008 | tf_op jit(solution)/shard_map/reduce_scatter | solution.py:109
  449.3 482.2 %copy-start = (bf16[512,2048]{1,0:T(8,128)(2,1)S(1)}, bf16[512,2048]{1,0:T(8,128)(2,1)}, u32[]{:S(2)}) copy-start(bf16[512,2048]{1,0:T(8,128)(2,1)} %param.6) | copy-start | bytes 6291460
Sparse Core Ops, SparseCore 0:
  9.7 72.8 all-gather.10
  84.7 66.8 all-gather.8
  153.7 66.8 all-gather.6
  222.5 66.8 all-gather.4
  293.0 156.3 reduce-scatter.10
  453.0 156.9 reduce-scatter.8
  613.7 156.9 reduce-scatter.6
  774.5 156.9 reduce-scatter.4
